TPU v7x, 512 devices: a whole 4x4x16 slice. The times are simulated.
512 devices in a mesh: shift: 8 (over x, core), batch: 16 (over z), cols: 4 (over y).
Axes of the slice: x: 4, y: 4, z: 16, core: 2. Of those that a mesh axis runs over, the one named last changes fastest.
Arguments:
- partial_up: float32 [128, 768, 3072], P(('shift', 'batch'), None, 'cols'), parts along dimension 0, may hold values from -0.875 to 0.875
- partial_down: float32 [128, 3072, 768], P(('shift', 'batch'), 'cols'), parts along dimension 0, may hold values from -0.875 to 0.875
- partial_norm: float32 [128, 768], P(('shift', 'batch')), parts along dimension 0, may hold values from -8 to 8
- partial_bias: float32 [128, 768], P(('shift', 'batch')), parts along dimension 0, may hold values from -8 to 8
- master_up: float32 [6144, 3072], P(('shift', 'batch'), 'cols'), parts along dimension 0, may hold values from -0.21875 to 0.21875
- master_down: float32 [24576, 768], P(('shift', 'cols'), 'batch'), parts along dimension 0, may hold values from -0.109375 to 0.109375
- master_norm: float32 [6144], P(('shift', 'batch')), parts along dimension 0, may hold values from 0.25 to 1.75
- master_bias: float32 [6144], P(('shift', 'batch')), parts along dimension 0, may hold values from -3 to 3
- memory_up: float32 [6144, 3072], P(('shift', 'batch'), 'cols'), parts along dimension 0, may hold values from -1.75 to 1.75
- memory_down: float32 [24576, 768], P(('shift', 'cols'), 'batch'), parts along dimension 0, may hold values from -1.75 to 1.75
- memory_norm: float32 [6144], P(('shift', 'batch')), parts along dimension 0, may hold values from -1.75 to 1.75
- memory_bias: float32 [6144], P(('shift', 'batch')), parts along dimension 0, may hold values from -1.75 to 1.75
Outputs:
- compute_up: bfloat16 [6144, 3072], P('shift', 'cols'), parts along dimension 0
- compute_down: bfloat16 [24576, 768], P(('shift', 'cols')), parts along dimension 0
- compute_norm: bfloat16 [6144], P('shift'), parts along dimension 0
- compute_bias: bfloat16 [6144], P('shift'), parts along dimension 0
- stepped_up: float32 [6144, 3072], P(('shift', 'batch'), 'cols'), parts along dimension 0
- stepped_down: float32 [24576, 768], P(('shift', 'cols'), 'batch'), parts along dimension 0
- stepped_norm: float32 [6144], P(('shift', 'batch')), parts along dimension 0
- stepped_bias: float32 [6144], P(('shift', 'batch')), parts along dimension 0
- state_new_up: float32 [6144, 3072], P(('shift', 'batch'), 'cols'), parts along dimension 0
- state_new_down: float32 [24576, 768], P(('shift', 'cols'), 'batch'), parts along dimension 0
- state_new_norm: float32 [6144], P(('shift', 'batch')), parts along dimension 0
- state_new_bias: float32 [6144], P(('shift', 'batch')), parts along dimension 0
There are 8 independent parts, one for each index of `shift`. A program takes and returns all parts, laid end to end along the dimension named above; each array names one. Nothing has to cross between parts.
All inputs are finite; a program needn't handle non-finite values.
Results may differ from a plain program's by a relative error of at most 0.0085.
Values may be sent and summed in bfloat16 or wider, within the bound.
No kernel may reach another device: no remote copies, remote signals or barrier semaphores. Data moves between devices by JAX's collectives and lax.ppermute only.
A program may use at most 64 MiB of HBM per device.

v0:
```python
import jax
import jax.numpy as jnp
from jax import lax
from jax.sharding import PartitionSpec as P

learn_rate = 0.1
hold_rate = 0.8


def in_blocks(array, dim, devices):
    shape = array.shape
    tiles = array.reshape(*shape[:dim], devices, shape[dim] // devices, *shape[dim + 1 :])
    return jnp.moveaxis(tiles, dim, 0)


def one_scatter(arrays, axis, dims):
    devices = lax.axis_size(axis)
    tiles = [in_blocks(a, dim, devices) for a, dim in zip(arrays, dims)]
    lines = jnp.concatenate([b.reshape(devices, -1) for b in tiles], axis=1)
    span = max(16, -(-lines.shape[1] // 1024) * 8)
    lines = jnp.pad(lines, ((0, 0), (0, span * 128 - lines.shape[1]))).reshape(-1, 128)
    line, at, finished = (lax.psum_scatter(lines, axis, tiled=True).reshape(-1), 0, [])
    for b in tiles:
        part = b[0]
        finished.append(line[at : at + part.size].reshape(part.shape))
        at += part.size
    return tuple(finished)


def sent_to_all(array, axis):
    copies = jnp.broadcast_to(array, (lax.axis_size(axis), *array.shape))
    return lax.all_to_all(copies, axis, split_axis=0, concat_axis=0, tiled=True)


def of_everyone(array, axis):
    return sent_to_all(array, axis).sum(axis=0)


def in_one(arrays, axis):
    line, at, finished = (jnp.concatenate([a.reshape(-1) for a in arrays]), 0, [])
    so_far = of_everyone(line, axis)
    for a in arrays:
        finished.append(so_far[at : at + a.size].reshape(a.shape))
        at += a.size
    return tuple(finished)


def gather_turned(arrays, axis, dims):
    turned = [jnp.moveaxis(a, dim, 0) for a, dim in zip(arrays, dims)]
    both = jnp.concatenate([t.reshape(len(t), -1) for t in turned], axis=1)
    filled, at, finished = (lax.all_gather(both, axis, axis=0, tiled=True), 0, [])
    for t, dim in zip(turned, dims):
        slab = filled[:, at : at + t[0].size].reshape(-1, *t.shape[1:])
        finished.append(jnp.moveaxis(slab, 0, dim))
        at += t[0].size
    return tuple(finished)


def on_device(
    partial_up,
    partial_down,
    partial_norm,
    partial_bias,
    master_up,
    master_down,
    master_norm,
    master_bias,
    memory_up,
    memory_down,
    memory_norm,
    memory_bias,
):
    mean_up, mean_down = tuple(
        (
            part.astype(jnp.float32)
            for part in one_scatter(
                (partial_up[0].astype(jnp.bfloat16), partial_down[0].astype(jnp.bfloat16)),
                "batch",
                (0, 1),
            )
        )
    )
    whole_norm, whole_bias = in_one((partial_norm[0], partial_bias[0]), "batch")
    place = lax.axis_index("batch")
    mean_norm = lax.dynamic_slice_in_dim(
        whole_norm, place * master_norm.shape[0], master_norm.shape[0]
    )
    mean_bias = lax.dynamic_slice_in_dim(
        whole_bias, place * master_bias.shape[0], master_bias.shape[0]
    )
    mean_rate = lax.axis_size("batch") ** (-0.5)
    mean_up = mean_up * mean_rate
    mean_down = mean_down * mean_rate
    mean_norm = mean_norm * mean_rate
    mean_bias = mean_bias * mean_rate
    state_new_up = hold_rate * memory_up + mean_up
    stepped_up = master_up - learn_rate * state_new_up
    state_new_down = hold_rate * memory_down + mean_down
    stepped_down = master_down - learn_rate * state_new_down
    state_new_norm = hold_rate * memory_norm + mean_norm
    stepped_norm = master_norm - learn_rate * state_new_norm
    state_new_bias = hold_rate * memory_bias + mean_bias
    stepped_bias = master_bias - learn_rate * state_new_bias
    compute_up, compute_down, compute_norm, compute_bias = gather_turned(
        (
            stepped_up.astype(jnp.bfloat16),
            stepped_down.astype(jnp.bfloat16),
            stepped_norm.astype(jnp.bfloat16),
            stepped_bias.astype(jnp.bfloat16),
        ),
        "batch",
        (0, 1, 0, 0),
    )
    return (
        compute_up,
        compute_down,
        compute_norm,
        compute_bias,
        stepped_up,
        stepped_down,
        stepped_norm,
        stepped_bias,
        state_new_up,
        state_new_down,
        state_new_norm,
        state_new_bias,
    )


def solution(mesh):
    return jax.shard_map(
        on_device,
        mesh=mesh,
        in_specs=(
            P(("shift", "batch"), None, "cols"),
            P(("shift", "batch"), "cols", None),
            P(("shift", "batch"), None),
            P(("shift", "batch"), None),
            P(("shift", "batch"), "cols"),
            P(("shift", "cols"), "batch"),
            P(("shift", "batch")),
            P(("shift", "batch")),
            P(("shift", "batch"), "cols"),
            P(("shift", "cols"), "batch"),
            P(("shift", "batch")),
            P(("shift", "batch")),
        ),
        out_specs=(
            P("shift", "cols"),
            P(("shift", "cols"), None),
            P("shift"),
            P("shift"),
            P(("shift", "batch"), "cols"),
            P(("shift", "cols"), "batch"),
            P(("shift", "batch")),
            P(("shift", "batch")),
            P(("shift", "batch"), "cols"),
            P(("shift", "cols"), "batch"),
            P(("shift", "batch")),
            P(("shift", "batch")),
        ),
        check_vma=False,
    )
```

profile of v0, /device:TPU:2, one launch (start us, length us, event | category | flops | bytes accessed | tf_op | source)
XLA Modules:
  0.0 193.8 jit_solution(17056441579653898916)
XLA Ops:
  7.2 0.0 reduce-scatter.2.cloned.1.call-start
  7.2 1.9 convert_element_type.34
  9.2 1.4 convert_element_type.35
  10.6 1.5 copy.50
  12.0 3.0 %copy.51 = bf16[16,768,48]{2,1,0:T(8,128)(2,1)S(1)} copy(bf16[16,768,48]{1,2,0:T(8,128)(2,1)} %bitcast.11) | data formatting | bytes 2359296 | tf_op jit(solution)/shard_map/transpose | solution.py:13
  15.0 7.1 %reshape.64 = bf16[16,36864]{1,0:T(8,128)(2,1)} reshape(bf16[16,768,48]{2,1,0:T(8,128)(2,1)S(1)} %copy.51) | data formatting | bytes 2359296 | tf_op jit(solution)/shard_map/reshape | solution.py:19
  22.2 1.8 pad_maximum_fusion
  23.9 2.1 %reshape.65 = bf16[9216,128]{1,0:T(8,128)(2,1)} reshape(bf16[16,73728]{1,0:T(8,128)(2,1)S(1)} %pad_maximum_fusion) | data formatting | bytes 4718592 | tf_op jit(solution)/shard_map/reshape | solution.py:21
  26.1 0.0 copy-start.10
  26.1 0.0 copy-start.1
  26.2 0.0 reduce-scatter.2.cloned.1.call-update
  26.2 0.6 copy-done.5
  26.8 0.7 broadcast_in_dim.3
  27.5 15.2 %all-to-all-start = ((f32[16,1,1536]{2,1,0:T(1,128)}), f32[16,1,1536]{2,1,0:T(1,128)S(1)}, u32[]{:S(2)}, u32[]{:S(2)}) async-start(f32[16,1,1536]{2,1,0:T(1,128)} %broadcast_in_dim.3), calls=%async_computation.1 | async-start | bytes 196608 | tf_op jit(solution)/shard_map/all_to_all | solution.py:32
  42.7 0.0 all-gather.2.cloned.1.call-start
  42.8 13.6 %all-to-all-done = f32[16,1,1536]{2,1,0:T(1,128)S(1)} async-done(((f32[16,1,1536]{2,1,0:T(1,128)}), f32[16,1,1536]{2,1,0:T(1,128)S(1)}, u32[]{:S(2)}, u32[]{:S(2)}) %all-to-all-start) | async-done | bytes 98336 | tf_op jit(solution)/shard_map/all_to_all | solution.py:32
  56.4 0.1 reduce_sum.9
  56.5 0.6 convert_bitcast_fusion.1
  57.1 0.1 copy.55
  57.2 0.1 copy.54
  57.3 48.8 %reduce-scatter.2.cloned.1.call-done = bf16[576,128]{1,0:T(8,128)(2,1)} async-done(((bf16[9216,128]{1,0:T(8,128)(2,1)}), bf16[576,128]{1,0:T(8,128)(2,1)}) %reduce-scatter.2.cloned.1.call-update) | async-done | bytes 147472 | tf_op jit(solution)/shard_map/reduce_scatter | solution.py:22
  106.1 0.9 convert_multiply_fusion
  107.1 0.2 mul.72
  107.3 0.1 copy.52
  107.4 0.7 fusion
  108.2 0.7 convert_bitcast_fusion
  108.9 0.8 concatenate.11
  109.7 0.0 all-gather.2.cloned.1.call-update
  109.7 71.1 %all-gather.2.cloned.1.call-done = bf16[768,1538]{1,0:T(8,128)(2,1)} async-done(((bf16[48,1538]{1,0:T(8,128)(2,1)}), bf16[768,1538]{1,0:T(8,128)(2,1)}) %all-gather.2.cloned.1.call-update) | async-done | bytes 2362384 | tf_op jit(solution)/shard_map/all_gather | solution.py:51
  180.8 2.8 %slice_bitcast_fusion = (bf16[768,768]{0,1:T(8,128)(2,1)S(1)}, bf16[768,768]{1,0:T(8,128)(2,1)}) fusion(bf16[768,1538]{1,0:T(8,128)(2,1)} %all-gather.2.cloned.1.call-done), kind=kLoop, calls=%fused_computation.1 | loop fusion | bytes 4718592 | tf_op jit(solution)/shard_map/transpose | solution.py:54
  183.6 1.4 copy.56
  185.0 1.9 slice_reduce_fusion
  (24 shorter events, 0.1 us)
Async XLA Ops:
  7.2 3.4 %copy-start = (f32[1,768,768]{2,1,0:T(8,128)S(1)}, f32[1,768,768]{2,1,0:T(8,128)}, u32[]{:S(2)}) copy-start(f32[1,768,768]{2,1,0:T(8,128)} %param.13) | copy-start | bytes 7077892
  7.2 98.9 %reduce-scatter.2.cloned.1.call-start = ((), (), s32[]{:S(2)}) async-start(), calls=%async_computation.2 | async-start | bytes 2506752 | tf_op jit(solution)/shard_map/reduce_scatter | solution.py:22
  26.1 0.7 copy-start.5
  26.1 0.7 copy-start.6
  26.1 30.4 %copy-start.7 = (f32[48]{0:T(128)S(1)}, f32[48]{0:T(128)}, u32[]{:S(2)}) copy-start(f32[48]{0:T(128)} %param.19) | copy-start | bytes 580
  26.1 30.4 %copy-start.8 = (f32[48]{0:T(128)S(1)}, f32[48]{0:T(128)}, u32[]{:S(2)}) copy-start(f32[48]{0:T(128)} %param.23) | copy-start | bytes 580
  26.1 30.4 %copy-start.9 = (f32[48]{0:T(128)S(1)}, f32[48]{0:T(128)}, u32[]{:S(2)}) copy-start(f32[48]{0:T(128)} %param.18) | copy-start | bytes 580
  26.1 30.4 %copy-start.10 = (f32[48]{0:T(128)S(1)}, f32[48]{0:T(128)}, u32[]{:S(2)}) copy-start(f32[48]{0:T(128)} %param.22) | copy-start | bytes 580
  26.1 81.3 %copy-start.1 = (f32[48,768]{1,0:T(8,128)S(1)}, f32[48,768]{1,0:T(8,128)}, u32[]{:S(2)}) copy-start(f32[48,768]{1,0:T(8,128)} %param.16) | copy-start | bytes 442372
  26.1 81.3 %copy-start.2 = (f32[48,768]{1,0:T(8,128)S(1)}, f32[48,768]{1,0:T(8,128)}, u32[]{:S(2)}) copy-start(f32[48,768]{1,0:T(8,128)} %param.20) | copy-start | bytes 442372
  26.1 82.0 %copy-start.3 = (f32[768,48]{0,1:T(8,128)S(1)}, f32[768,48]{0,1:T(8,128)}, u32[]{:S(2)}) copy-start(f32[768,48]{0,1:T(8,128)} %param.17) | copy-start | bytes 442372
  26.2 82.0 %copy-start.4 = (f32[768,48]{0,1:T(8,128)S(1)}, f32[768,48]{0,1:T(8,128)}, u32[]{:S(2)}) copy-start(f32[768,48]{0,1:T(8,128)} %param.21) | copy-start | bytes 442372
  27.5 28.9 %all-to-all-start = ((f32[16,1,1536]{2,1,0:T(1,128)}), f32[16,1,1536]{2,1,0:T(1,128)S(1)}, u32[]{:S(2)}, u32[]{:S(2)}) async-start(f32[16,1,1536]{2,1,0:T(1,128)} %broadcast_in_dim.3), calls=%async_computation.1 | async-start | bytes 196608 | tf_op jit(solution)/shard_map/all_to_all | solution.py:32
  42.7 138.1 %all-gather.2.cloned.1.call-start = ((), (), s32[]{:S(2)}) async-start(), calls=%async_computation.3 | async-start | bytes 2715648 | tf_op jit(solution)/shard_map/all_gather | solution.py:51
Sparse Core Ops, SparseCore 0:
  26.3 79.7 reduce-scatter.1
  109.8 70.9 all-gather.1
where the time goes:
time: 194 us
  waiting for transfers between devices  134 us (69%)
  local copies, waits for them, and re-layouts  23.9 us (12%)
  starting transfers between devices  15.3 us (8%)
  between operations  14.2 us (7%)
  other arithmetic  6.85 us (4%)
    all_gather x1, waiting for transfers between devices, gather_turned(): lax.all_gather(both, axis, axis=0, tiled=True)  71.1 us
    reduce_scatter x1, waiting for transfers between devices, one_scatter(): lax.psum_scatter(lines, axis, tiled=True).reshape(-1)  48.8 us
    all_to_all x1, starting transfers between devices, sent_to_all(): return lax.all_to_all(copies, axis, split_axis=0, concat_axis=0, tiled=True)  15.2 us
    all_to_all x1, waiting for transfers between devices, sent_to_all(): return lax.all_to_all(copies, axis, split_axis=0, concat_axis=0, tiled=True)  13.6 us
    reshape x1, local copies, waits for them, and re-layouts, one_scatter(): lines = jnp.concatenate([b.reshape(devices, -1) for b in tiles], axis=1)  7.14 us
  transfers between devices with their start and end apart: 3, of which 3 were waited for; matrix products, arithmetic and copies ran while one was open for 1% of the time, Pallas kernels for 0%

commit v1 on v0

--- a/solution.py
+++ b/solution.py
@@ -48,7 +48,16 @@
 def gather_turned(arrays, axis, dims):
     turned = [jnp.moveaxis(a, dim, 0) for a, dim in zip(arrays, dims)]
     both = jnp.concatenate([t.reshape(len(t), -1) for t in turned], axis=1)
-    filled, at, finished = (lax.all_gather(both, axis, axis=0, tiled=True), 0, [])
+    filled, at, finished = (
+        jnp.concatenate(
+            jax.lax.all_to_all(
+                jnp.stack([both for _ in range(jax.lax.axis_size(axis))]), axis, 0, 0
+            ),
+            axis=0,
+        ),
+        0,
+        [],
+    )
     for t, dim in zip(turned, dims):
         slab = filled[:, at : at + t[0].size].reshape(-1, *t.shape[1:])
         finished.append(jnp.moveaxis(slab, 0, dim))

time: 194 us -> 235 us (1.21)
  the two profiles are of different devices: /device:TPU:2 before, /device:TPU:46 now
where the time goes in v1:
time: 235 us; the launch traced here: 234 us
  blocking collectives  116 us (49%)
  waiting for transfers between devices  61 us (26%)
  local copies, waits for them, and re-layouts  20.7 us (9%)
  starting transfers between devices  15.2 us (6%)
  between operations  14.2 us (6%)
  other arithmetic  6.85 us (3%)
    all_to_all x1, blocking collectives, gather_turned(): jax.lax.all_to_all(jnp.stack([both for _ in range(jax.lax.axis_size(axis)...  116 us
    reduce_scatter x1, waiting for transfers between devices, one_scatter(): lax.psum_scatter(lines, axis, tiled=True).reshape(-1)  48 us
    all_to_all x1, starting transfers between devices, sent_to_all(): return lax.all_to_all(copies, axis, split_axis=0, concat_axis=0, tiled=True)  15.2 us
    all_to_all x1, waiting for transfers between devices, sent_to_all(): return lax.all_to_all(copies, axis, split_axis=0, concat_axis=0, tiled=True)  13 us
    reshape x1, local copies, waits for them, and re-layouts, one_scatter(): lines = jnp.concatenate([b.reshape(devices, -1) for b in tiles], axis=1)  7.14 us
  transfers between devices with their start and end apart: 2, of which 2 were waited for; matrix products, arithmetic and copies ran while one was open for 1% of the time, Pallas kernels for 0%

profile of v1, /device:TPU:46, one launch (start us, length us, event | category | flops | bytes accessed | tf_op | source)
XLA Modules:
  0.0 234.3 jit_solution(6543196915028198705)
XLA Ops:
  7.2 0.0 reduce-scatter.2.cloned.1.call-start
  7.2 1.9 convert_element_type.34
  9.2 1.4 convert_element_type.35
  10.6 1.5 copy.52
  12.0 3.0 %copy.53 = bf16[16,768,48]{2,1,0:T(8,128)(2,1)S(1)} copy(bf16[16,768,48]{1,2,0:T(8,128)(2,1)} %bitcast.14) | data formatting | bytes 2359296 | tf_op jit(solution)/shard_map/transpose | solution.py:13
  15.0 7.1 %reshape.69 = bf16[16,36864]{1,0:T(8,128)(2,1)} reshape(bf16[16,768,48]{2,1,0:T(8,128)(2,1)S(1)} %copy.53) | data formatting | bytes 2359296 | tf_op jit(solution)/shard_map/reshape | solution.py:19
  22.2 1.8 pad_maximum_fusion
  23.9 2.1 reshape.70
  26.1 0.0 copy-start.9
  26.1 0.0 copy-start.10
  26.1 0.0 copy-start.3
  26.2 0.0 reduce-scatter.2.cloned.1.call-update
  26.2 0.6 copy-done.5
  26.8 0.7 broadcast_in_dim.3
  27.5 15.2 %all-to-all-start = ((f32[16,1,1536]{2,1,0:T(1,128)}), f32[16,1,1536]{2,1,0:T(1,128)S(1)}, u32[]{:S(2)}, u32[]{:S(2)}) async-start(f32[16,1,1536]{2,1,0:T(1,128)} %broadcast_in_dim.3), calls=%async_computation.1 | async-start | bytes 196608 | tf_op jit(solution)/shard_map/all_to_all | solution.py:32
  42.7 13.0 %all-to-all-done = f32[16,1,1536]{2,1,0:T(1,128)S(1)} async-done(((f32[16,1,1536]{2,1,0:T(1,128)}), f32[16,1,1536]{2,1,0:T(1,128)S(1)}, u32[]{:S(2)}, u32[]{:S(2)}) %all-to-all-start) | async-done | bytes 98336 | tf_op jit(solution)/shard_map/all_to_all | solution.py:32
  55.8 0.1 reduce_sum.9
  55.9 0.6 convert_bitcast_fusion.1
  56.5 0.1 copy.57
  56.6 0.1 copy.56
  56.7 48.0 %reduce-scatter.2.cloned.1.call-done = bf16[576,128]{1,0:T(8,128)(2,1)} async-done(((bf16[9216,128]{1,0:T(8,128)(2,1)}), bf16[576,128]{1,0:T(8,128)(2,1)}) %reduce-scatter.2.cloned.1.call-update) | async-done | bytes 147472 | tf_op jit(solution)/shard_map/reduce_scatter | solution.py:22
  104.7 0.9 convert_multiply_fusion
  105.7 0.2 mul.72
  105.8 0.1 copy.54
  106.0 0.7 fusion
  106.7 0.7 convert_bitcast_fusion
  107.5 0.1 concatenate.11
  107.6 0.2 stack.2
  107.8 116.2 %all_to_all.11 = bf16[16,48,1538]{2,1,0:T(8,128)(2,1)S(1)} all-to-all(bf16[16,48,1538]{2,1,0:T(8,128)(2,1)S(1)} %stack.2), channel_id=1, replica_groups=mesh['shift'=8,'batch'=16,'cols'=4] {'batch'}, dimensions={0} | all-to-all | bytes 4724736 | tf_op jit(solution)/shard_map/all_to_all | solution.py:53
  224.0 0.9 slice_reduce_fusion
  224.9 1.2 slice_bitcast_fusion
  226.0 1.4 copy.58
  (23 shorter events, 0.1 us)
Async XLA Ops:
  7.2 3.4 %copy-start = (f32[1,768,768]{2,1,0:T(8,128)S(1)}, f32[1,768,768]{2,1,0:T(8,128)}, u32[]{:S(2)}) copy-start(f32[1,768,768]{2,1,0:T(8,128)} %param.13) | copy-start | bytes 7077892
  7.2 97.5 %reduce-scatter.2.cloned.1.call-start = ((), (), s32[]{:S(2)}) async-start(), calls=%async_computation.3 | async-start | bytes 2506752 | tf_op jit(solution)/shard_map/reduce_scatter | solution.py:22
  26.1 0.7 copy-start.5
  26.1 0.7 copy-start.6
  26.1 29.8 %copy-start.7 = (f32[48]{0:T(128)S(1)}, f32[48]{0:T(128)}, u32[]{:S(2)}) copy-start(f32[48]{0:T(128)} %param.19) | copy-start | bytes 580
  26.1 29.8 %copy-start.8 = (f32[48]{0:T(128)S(1)}, f32[48]{0:T(128)}, u32[]{:S(2)}) copy-start(f32[48]{0:T(128)} %param.23) | copy-start | bytes 580
  26.1 29.8 %copy-start.9 = (f32[48]{0:T(128)S(1)}, f32[48]{0:T(128)}, u32[]{:S(2)}) copy-start(f32[48]{0:T(128)} %param.18) | copy-start | bytes 580
  26.1 29.8 %copy-start.10 = (f32[48]{0:T(128)S(1)}, f32[48]{0:T(128)}, u32[]{:S(2)}) copy-start(f32[48]{0:T(128)} %param.22) | copy-start | bytes 580
  26.1 79.9 %copy-start.1 = (f32[48,768]{1,0:T(8,128)S(1)}, f32[48,768]{1,0:T(8,128)}, u32[]{:S(2)}) copy-start(f32[48,768]{1,0:T(8,128)} %param.16) | copy-start | bytes 442372
  26.1 79.9 %copy-start.2 = (f32[48,768]{1,0:T(8,128)S(1)}, f32[48,768]{1,0:T(8,128)}, u32[]{:S(2)}) copy-start(f32[48,768]{1,0:T(8,128)} %param.20) | copy-start | bytes 442372
  26.1 80.6 %copy-start.3 = (f32[768,48]{0,1:T(8,128)S(1)}, f32[768,48]{0,1:T(8,128)}, u32[]{:S(2)}) copy-start(f32[768,48]{0,1:T(8,128)} %param.17) | copy-start | bytes 442372
  26.1 80.6 %copy-start.4 = (f32[768,48]{0,1:T(8,128)S(1)}, f32[768,48]{0,1:T(8,128)}, u32[]{:S(2)}) copy-start(f32[768,48]{0,1:T(8,128)} %param.21) | copy-start | bytes 442372
  27.5 28.3 %all-to-all-start = ((f32[16,1,1536]{2,1,0:T(1,128)}), f32[16,1,1536]{2,1,0:T(1,128)S(1)}, u32[]{:S(2)}, u32[]{:S(2)}) async-start(f32[16,1,1536]{2,1,0:T(1,128)} %broadcast_in_dim.3), calls=%async_computation.1 | async-start | bytes 196608 | tf_op jit(solution)/shard_map/all_to_all | solution.py:32
Sparse Core Ops, SparseCore 0:
  26.3 78.3 reduce-scatter.1
